TPU v7x, 256 devices: a whole 4x4x8 slice. The times are simulated.
256 devices in a mesh: dom: 128 (over x, z, y), mem: 2 (over core).
Axes of the slice: x: 4, y: 4, z: 8, core: 2. Of those that a mesh axis runs over, the one named last changes fastest.
Arguments:
- node_latents: bfloat16 [4, 16384, 512], P('mem', 'dom'), may hold values from -6 to 6
- edge_latents: bfloat16 [4, 65536, 512], P('mem', 'dom'), may hold values from -6 to 6
- edge_senders: int32 [65536], P('dom'), may hold values from 0 to 415, as said below
- edge_receivers: int32 [65536], P('dom'), may hold values from 0 to 127
- edge_counts: int32 [128], P('dom'), may hold values from 64 to 512, as said below
- halo_send: int32 [4096], P('dom'), may hold values from 0 to 127
- long_send: int32 [128, 128, 2], replicated, may hold values from 0 to 3
- edge_first: bfloat16 [2, 1536, 512], P(None, None, 'mem'), may hold values from -0.15625 to 0.15625
- edge_second: bfloat16 [2, 512, 512], P(None, None, 'mem'), may hold values from -0.25 to 0.25
- node_first: bfloat16 [2, 1024, 512], P(None, None, 'mem'), may hold values from -0.1875 to 0.1875
- node_second: bfloat16 [2, 512, 512], P(None, None, 'mem'), may hold values from -0.25 to 0.25
- edge_gain: float32 [2, 512], replicated, may hold values from 0.5 to 1.5
- edge_shift: float32 [2, 512], replicated, may hold values from -3 to 3
- node_gain: float32 [2, 512], replicated, may hold values from 0.5 to 1.5
- node_shift: float32 [2, 512], replicated, may hold values from -3 to 3
Outputs:
- node_out: bfloat16 [4, 16384, 512], P('mem', 'dom')
- edge_out: bfloat16 [4, 65536, 512], P('mem', 'dom')
Inputs may be any that keep to these rules, and one draw needn't show every extreme that they name: `edge_senders`: rows below 128 are the partition's own nodes, the next 32 its neighbours' sent nodes, the rest the coarse slots of all partitions. `edge_counts`: live slots come first in each partition; some partition has exactly 512 live slots.
All inputs are finite; a program needn't handle non-finite values.
Results may differ from a plain program's by a relative error of at most 0.0075.
Values may be sent and summed in bfloat16 or wider, within the bound.
A program may use at most 128 MiB of HBM per device.

v0:
```python
import functools

import jax
import jax.numpy as jnp
from jax import lax
from jax.experimental import pallas as pl
from jax.experimental.pallas import tpu as pltpu
from jax.sharding import PartitionSpec as P

NX, NZ, NY = 4, 8, 4
HALO = 16
LAYERS = 2
COARSE = 4
MESH = pl.DeviceIdType.MESH
F32 = jnp.float32
BF16 = jnp.bfloat16
RING = sorted(range(1, NZ), key=lambda d: -min(d, NZ - d))
PLANE = sorted(
    [(i, j) for i in range(NX) for j in range(NY) if (i, j) != (0, 0)],
    key=lambda o: -(min(o[0], NX - o[0]) + min(o[1], NY - o[1])),
)


def dot(a, b):
    return jnp.dot(a, b, preferred_element_type=F32)


def silu(x):
    half = 0.5 * x
    return half * jnp.tanh(half) + half


def kernel(
    dims,
    count_ref,
    senders_ref,
    receivers_ref,
    halo_ref,
    pick_ref,
    eg_ref,
    eb_ref,
    ng_ref,
    nb_ref,
    node_hbm,
    edge_hbm,
    ef_hbm,
    es_hbm,
    nf_hbm,
    ns_hbm,
    node_out,
    edge_out,
    node_v,
    edge_v,
    w1e,
    w2e,
    w1n,
    w2n,
    near_rows,
    far_rows,
    ring_send,
    ring_recv,
    plane_send,
    halo_out,
    o_near,
    o_far,
    o_recv,
    o_sum,
    o_pick,
    o_pack,
    pre_v,
    hid_v,
    load_sem,
    out_sem,
    w_send,
    w_recv,
    ring_ssem,
    ring_rsem,
    plane_ssem,
    plane_rsem,
    halo_ssem,
    halo_rsem,
):
    M, N, E, D = dims
    H = D // 2
    K = N + 2 * HALO
    dom = lax.axis_index("dom")
    mem = lax.axis_index("mem")
    y = lax.rem(dom, NY)
    z = lax.rem(lax.div(dom, NY), NZ)
    x = lax.div(dom, NY * NZ)

    def dom_of(a, b, c):
        return (a * NZ + b) * NY + c

    def along(d):
        return (dom_of(x, lax.rem(z + d, NZ), y), mem)

    def across(o):
        return (dom_of(lax.rem(x + o[0], NX), z, lax.rem(y + o[1], NY)), mem)

    nd = NX * NY * NZ
    after = (lax.rem(dom + 1, nd), mem)
    before = (lax.rem(dom + nd - 1, nd), mem)
    twin = (dom, 1 - mem)
    here = x * NY + y
    peers = [along(d) for d in RING] + [across(o) for o in PLANE] + [after, before, twin]
    barrier = pltpu.get_barrier_semaphore()
    for p in peers:
        pl.semaphore_signal(barrier, inc=1, device_id=p, device_id_type=MESH)

    weights = ((ef_hbm, w1e), (es_hbm, w2e), (nf_hbm, w1n), (ns_hbm, w2n))
    node_load = pltpu.make_async_copy(node_hbm, node_v, load_sem.at[0])
    edge_load = pltpu.make_async_copy(edge_hbm, edge_v, load_sem.at[1])
    node_load.start()
    w_load = {}
    for l in range(LAYERS):
        for i, (src, dst) in enumerate(weights):
            w_load[l, i] = pltpu.make_async_copy(
                src.at[l], dst.at[l, mem], load_sem.at[2 + 4 * l + i]
            )
            w_load[l, i].start()
            if l == 0 and i == 0:
                edge_load.start()

    live = count_ref[0]
    table = lax.broadcasted_iota(jnp.int32, (K, E), 0)
    sent = senders_ref[...]
    o_near[...] = jnp.where(table == sent, 1.0, 0.0).T.astype(BF16)
    q = jnp.maximum(sent - K, 0)
    slot = lax.rem(q, 2)
    part = lax.div(q, 2)
    part_y = lax.rem(part, NY)
    part_z = lax.rem(lax.div(part, NY), NZ)
    part_x = lax.div(part, NY * NZ)
    place = jnp.where(
        sent >= K, (part_x * NY + part_y) * (2 * NZ) + part_z * 2 + slot, -1
    )
    F = 2 * nd
    table = lax.broadcasted_iota(jnp.int32, (F, E), 0)
    o_far[...] = jnp.where(table == place, 1.0, 0.0).T.astype(BF16)
    table = lax.broadcasted_iota(jnp.int32, (N, E), 0)
    lane = lax.broadcasted_iota(jnp.int32, (N, E), 1)
    got = jnp.where((table == receivers_ref[...]) & (lane < live), 1.0, 0.0)
    o_sum[...] = got.astype(BF16)
    o_recv[...] = got.T.astype(BF16)
    row = lax.broadcasted_iota(jnp.int32, (N, 2 * HALO), 0)
    halo = jnp.where(row == halo_ref[...], 1.0, 0.0).T
    row = lax.broadcasted_iota(jnp.int32, (8, N), 0)
    col = lax.broadcasted_iota(jnp.int32, (8, N), 1)
    o_pack[0] = jnp.where(row == col, jnp.where(row < COARSE, 1.0, 0.0), 0.0).astype(BF16)
    o_pack[1] = jnp.where(row == col + COARSE, 1.0, 0.0).astype(BF16)
    o_halo = halo.astype(BF16)
    G = NX * NY * 2 * NZ
    table = lax.broadcasted_iota(jnp.int32, (8 * NZ, G), 0)
    o_pick[0] = jnp.where(table == pick_ref[...], 1.0, 0.0).T.astype(BF16)
    o_pick[1] = jnp.where(table == pick_ref[...] + COARSE, 1.0, 0.0).T.astype(BF16)

    def ring_copy(l, m, d):
        return pltpu.make_async_remote_copy(
            src_ref=ring_send.at[l, m],
            dst_ref=ring_recv.at[l, m, z],
            send_sem=ring_ssem.at[l, m, d],
            recv_sem=ring_rsem.at[l, m, d],
            device_id=along(d),
            device_id_type=MESH,
        )

    def plane_copy(l, m, k):
        o = PLANE[k]
        there = lax.rem(x + o[0], NX) * NY + lax.rem(y + o[1], NY)
        return pltpu.make_async_remote_copy(
            src_ref=plane_send.at[l, m, there],
            dst_ref=far_rows.at[l, m, here],
            send_sem=plane_ssem.at[l, m, k],
            recv_sem=plane_rsem.at[l, m, k],
            device_id=across(o),
            device_id_type=MESH,
        )

    def halo_copy(l, m, side):
        return pltpu.make_async_remote_copy(
            src_ref=halo_out.at[l, m, side],
            dst_ref=near_rows.at[l, m, pl.ds(N + (1 - side) * HALO, HALO)],
            send_sem=halo_ssem.at[l, m, side],
            recv_sem=halo_rsem.at[l, m, side],
            device_id=before if side == 0 else after,
            device_id_type=MESH,
        )

    def weight_copy(l, i):
        src, dst = weights[i]
        return pltpu.make_async_remote_copy(
            src_ref=src.at[l],
            dst_ref=dst.at[l, mem],
            send_sem=w_send.at[l, i],
            recv_sem=w_recv.at[l, i],
            device_id=twin,
            device_id_type=MESH,
        )

    def pack(l, m):
        rows = near_rows[l, m, 0:N]
        ring_send[l, m] = (
            dot(o_pack[0], rows[:, 0:H]) + dot(o_pack[1], rows[:, H:D])
        ).astype(BF16)
        return rows

    def halo_pack(l, m, rows):
        out = dot(o_halo, rows).astype(BF16)
        halo_out[l, m, 0] = out[0:HALO]
        halo_out[l, m, 1] = out[HALO : 2 * HALO]

    def ring_start(l, m):
        ring_recv[l, m, z] = ring_send[l, m]
        for d in RING:
            ring_copy(l, m, d).start()

    def halo_start(l, m):
        for side in range(2):
            halo_copy(l, m, side).start()

    def forward(l, m):
        for d in RING:
            ring_copy(l, m, d).wait_recv()
        got = ring_recv[l, m].reshape(8 * NZ, H)
        for h in range(2):
            plane_send[l, m, :, :, h * H : (h + 1) * H] = (
                dot(o_pick[h], got).astype(BF16).reshape(NX * NY, 2 * NZ, H)
            )
        for k in range(len(PLANE)):
            plane_copy(l, m, k).start()
        far_rows[l, m, here] = plane_send[l, m, here]

    def halo_wait(l, m):
        for side in range(2):
            halo_copy(l, m, side).wait_recv()

    def near(l, m):
        rows = near_rows[l, m]
        for n in range(2):
            cols = slice(n * H, (n + 1) * H)
            proj = dot(rows, w1e[l, n, D : 2 * D]).astype(BF16)
            own = dot(rows[0:N], w1e[l, n, 2 * D : 3 * D]).astype(BF16)
            pre_v[m, :, cols] = (
                dot(edge_v[m], w1e[l, n, 0:D])
                + dot(o_near[...], proj)
                + dot(o_recv[...], own)
            )

    def norm(v, gain, shift):
        mean = jnp.mean(v, -1, keepdims=True)
        c = v - mean
        var = jnp.mean(c * c, -1, keepdims=True)
        return c * lax.rsqrt(var + 1e-05) * gain + shift

    CH = min(256, E)

    def edges(l, m):
        for k in range(len(PLANE)):
            plane_copy(l, m, k).wait_recv()
        rows = far_rows[l, m].reshape(F, D)
        for n in range(2):
            cols = slice(n * H, (n + 1) * H)
            proj = dot(rows, w1e[l, n, D : 2 * D]).astype(BF16)
            for c in range(E // CH):
                r = slice(c * CH, (c + 1) * CH)
                hid_v[r, cols] = silu(pre_v[m, r, cols] + dot(o_far[r], proj)).astype(BF16)
        gain = eg_ref[l : l + 1]
        shift = eb_ref[l : l + 1]
        for c in range(E // CH):
            r = slice(c * CH, (c + 1) * CH)
            h = hid_v[r]
            v = jnp.concatenate([dot(h, w2e[l, 0]), dot(h, w2e[l, 1])], -1)
            u = norm(v, gain, shift)
            at = lax.broadcasted_iota(jnp.int32, (CH, 1), 0) + c * CH
            edge_v[m, r] = jnp.where(
                at < live, edge_v[m, r].astype(F32) + u, 0.0
            ).astype(BF16)

    def nodes(l, m):
        summed = dot(o_sum[...], edge_v[m]).astype(BF16)
        rows = near_rows[l, m, 0:N]
        hid = []
        for n in range(2):
            a = dot(rows, w1n[l, n, 0:D]) + dot(summed, w1n[l, n, D : 2 * D])
            hid.append(silu(a).astype(BF16))
        h = jnp.concatenate(hid, -1)
        v = jnp.concatenate([dot(h, w2n[l, 0]), dot(h, w2n[l, 1])], -1)
        u = norm(v, ng_ref[l : l + 1], nb_ref[l : l + 1])
        return (rows.astype(F32) + u).astype(BF16)

    node_load.wait()
    for m in range(M):
        near_rows[0, m, 0:N] = node_v[m]
        rows = pack(0, m)
        halo_pack(0, m, rows)
    pl.semaphore_wait(barrier, len(peers))
    for m in range(M):
        ring_start(0, m)
    for m in range(M):
        halo_start(0, m)
    for l in range(LAYERS):
        for i in range(4):
            weight_copy(l, i).start()
    for m in range(M):
        forward(0, m)
    edge_load.wait()
    for l in range(LAYERS):
        for i in range(4):
            if l == 0:
                w_load[l, i].wait()
    weight_copy(0, 0).wait_recv()
    for m in range(M):
        halo_wait(0, m)
        near(0, m)
    for i in range(1, 4):
        weight_copy(0, i).wait_recv()
    for m in range(M):
        edges(0, m)
        new = nodes(0, m)
        near_rows[1, m, 0:N] = new
        rows = pack(1, m)
        ring_start(1, m)
        halo_pack(1, m, rows)
        halo_start(1, m)
    for i in range(4):
        w_load[1, i].wait()
        weight_copy(1, i).wait_recv()
    halo_wait(1, 0)
    near(1, 0)
    forward(1, 0)
    halo_wait(1, 1)
    near(1, 1)
    forward(1, 1)
    outs = []
    for m in range(M):
        edges(1, m)
        out = pltpu.make_async_copy(edge_v.at[m], edge_out.at[m], out_sem.at[m, 0])
        out.start()
        outs.append(out)
        node_v[m] = nodes(1, m)
        out = pltpu.make_async_copy(node_v.at[m], node_out.at[m], out_sem.at[m, 1])
        out.start()
        outs.append(out)
    for l in range(LAYERS):
        for i in range(4):
            weight_copy(l, i).wait_send()
        for m in range(M):
            for d in RING:
                ring_copy(l, m, d).wait_send()
            for k in range(len(PLANE)):
                plane_copy(l, m, k).wait_send()
            for side in range(2):
                halo_copy(l, m, side).wait_send()
    for out in outs:
        out.wait()


def per_device(
    node_latents,
    edge_latents,
    edge_senders,
    edge_receivers,
    edge_counts,
    halo_send,
    long_send,
    edge_first,
    edge_second,
    node_first,
    node_second,
    edge_gain,
    edge_shift,
    node_gain,
    node_shift,
):
    M, N, D = node_latents.shape
    E = edge_latents.shape[1]
    H = D // 2
    L = LAYERS
    nd = NX * NY * NZ
    K = N + 2 * HALO
    F = 2 * nd
    G = NX * NY * 2 * NZ
    dom = lax.axis_index("dom")
    y = lax.rem(dom, NY)
    z = lax.rem(lax.div(dom, NY), NZ)
    x = lax.div(dom, NY * NZ)
    sent = long_send.transpose(0, 2, 1).reshape(NX, NZ, NY, 2, NX, NZ, NY)
    sent = lax.dynamic_slice(
        sent, (x, 0, y, 0, 0, z, 0), (1, NZ, 1, 2, NX, 1, NY)
    ).reshape(NZ, 2, NX * NY)
    pick = sent.transpose(2, 0, 1) + 8 * jnp.arange(NZ, dtype=jnp.int32)[None, :, None]
    pick = pick.reshape(1, G)
    vmem = pl.BlockSpec(memory_space=pltpu.VMEM)
    smem = pl.BlockSpec(memory_space=pltpu.SMEM)
    hbm = pl.BlockSpec(memory_space=pl.ANY)
    DMA = pltpu.SemaphoreType.DMA
    return pl.pallas_call(
        functools.partial(kernel, (M, N, E, D)),
        out_shape=(
            jax.ShapeDtypeStruct((M, N, D), BF16),
            jax.ShapeDtypeStruct((M, E, D), BF16),
        ),
        in_specs=[smem] + [vmem] * 8 + [hbm] * 6,
        out_specs=(hbm, hbm),
        scratch_shapes=[
            pltpu.VMEM((M, N, D), BF16),
            pltpu.VMEM((M, E, D), BF16),
            pltpu.VMEM((L, 2, 3 * D, H), BF16),
            pltpu.VMEM((L, 2, D, H), BF16),
            pltpu.VMEM((L, 2, 2 * D, H), BF16),
            pltpu.VMEM((L, 2, D, H), BF16),
            pltpu.VMEM((L, M, K, D), BF16),
            pltpu.VMEM((L, M, NX * NY, 2 * NZ, D), BF16),
            pltpu.VMEM((L, M, 8, H), BF16),
            pltpu.VMEM((L, M, NZ, 8, H), BF16),
            pltpu.VMEM((L, M, NX * NY, 2 * NZ, D), BF16),
            pltpu.VMEM((L, M, 2, HALO, D), BF16),
            pltpu.VMEM((E, K), BF16),
            pltpu.VMEM((E, F), BF16),
            pltpu.VMEM((E, N), BF16),
            pltpu.VMEM((N, E), BF16),
            pltpu.VMEM((2, G, 8 * NZ), BF16),
            pltpu.VMEM((2, 8, N), BF16),
            pltpu.VMEM((M, E, D), F32),
            pltpu.VMEM((E, D), BF16),
            DMA((2 + 4 * L,)),
            DMA((M, 2)),
            DMA((L, 4)),
            DMA((L, 4)),
            DMA((L, M, NZ)),
            DMA((L, M, NZ)),
            DMA((L, M, len(PLANE))),
            DMA((L, M, len(PLANE))),
            DMA((L, M, 2)),
            DMA((L, M, 2)),
        ],
        compiler_params=pltpu.CompilerParams(
            collective_id=0, has_side_effects=True, vmem_limit_bytes=56 * 1024 * 1024
        ),
    )(
        edge_counts,
        edge_senders.reshape(1, E),
        edge_receivers.reshape(1, E),
        halo_send.reshape(1, 2 * HALO),
        pick,
        edge_gain,
        edge_shift,
        node_gain,
        node_shift,
        node_latents,
        edge_latents,
        edge_first,
        edge_second,
        node_first,
        node_second,
    )


def solution(mesh):
    placed = (
        P("mem", "dom", None),
        P("mem", "dom", None),
        P("dom"),
        P("dom"),
        P("dom"),
        P("dom"),
        P(),
        P(None, None, "mem"),
        P(None, None, "mem"),
        P(None, None, "mem"),
        P(None, None, "mem"),
        P(),
        P(),
        P(),
        P(),
    )
    return jax.shard_map(
        per_device,
        mesh=mesh,
        in_specs=placed,
        out_specs=(P("mem", "dom", None), P("mem", "dom", None)),
        check_vma=False,
    )
```

profile of v0, /device:TPU:2, one launch (start us, length us, event | category | flops | bytes accessed | tf_op | source)
XLA Modules:
  0.0 55.4 jit_solution(9547023486912031765)
XLA Ops:
  1.3 0.9 %copy.19 = s32[128,2,128]{2,0,1:T(8,128)S(1)} copy(s32[128,2,128]{2,1,0:T(2,128)} %bitcast.9) | data formatting | bytes 262144 | tf_op jit(solution)/shard_map/transpose | solution.py:388
  2.2 5.7 %reshape.30 = s32[4,8,4,2,4,8,4]{6,5,4,2,1,0,3:T(8,128)} reshape(s32[128,2,128]{2,0,1:T(8,128)S(1)} %copy.19) | data formatting | bytes 262144 | tf_op jit(solution)/shard_map/reshape | solution.py:388
  7.8 1.0 %constant_dynamic-slice_fusion = s32[1,8,1,2,4,1,4]{6,5,4,2,1,0,3:T(1,128)S(1)} fusion(s32[4,8,4,2,4,8,4]{6,5,4,2,1,0,3:T(8,128)} %reshape.30, s32[]{:T(128)S(6)} %select_n.9, s32[]{:T(128)S(6)} %select_n.10, s32[]{:T(128)S(6)} %select_n.11), kind=kLoop, calls=%fused_computation.2 | loop fusion | bytes 2060 | tf_op jit(solution)/shard_map/dynamic_slice | solution.py:389
  8.8 0.1 copy.20
  9.0 0.2 copy.21
  9.1 0.7 %reshape.32.pick_ref = s32[1,256]{1,0:T(1,128)} reshape(s32[16,8,2]{2,1,0:T(8,128)S(1)} %copy.21) | data formatting | bytes 2048 | tf_op jit(solution)/shard_map/reshape | solution.py:393
  9.8 41.6 %shard_map.158 = (bf16[2,128,512]{2,1,0:T(8,128)(2,1)}, bf16[2,512,512]{2,1,0:T(8,128)(2,1)}) custom-call(s32[1]{0:T(128)S(6)} %copy.24.count_ref, s32[1,512]{1,0:T(1,128)} %bitcast.11, s32[1,512]{1,0:T(1,128)} %bitcast.12, s32[1,32]{1,0:T(1,128)} %bitcast.13, s32[1,256]{1,0:T(1,128)} %reshape.32.pick_ref, f32[2,512]{1,0:T(2,128)} %eg_ref.1, ...), custom_call_target="tpu_custom_call" | custom-call | tf_op jit(solution)/shard_map/pallas_call | solution.py:398
  51.4 1.7 %copy.25 = bf16[2,128,512]{2,1,0:T(8,128)(2,1)} copy(bf16[2,128,512]{2,1,0:T(8,128)(2,1)} %get-tuple-element.4) | data formatting | bytes 524288
  53.1 2.3 %copy.26 = bf16[2,512,512]{2,1,0:T(8,128)(2,1)} copy(bf16[2,512,512]{2,1,0:T(8,128)(2,1)} %get-tuple-element.5) | data formatting | bytes 2097152
  (2 shorter events, 0.0 us)
where the time goes:
time: 55.6 us; the launch traced here: 55.4 us
  Pallas kernels  41.6 us (75%)
  local copies, waits for them, and re-layouts  12.5 us (22%)
  between operations  1.29 us (2%)
    pallas_call x1, Pallas kernels, per_device(): pl.pallas_call(functools.partial(kernel, (M, N, E, D)), out_shape=(jax.Sh...  41.6 us
    reshape x1, local copies, waits for them, and re-layouts, per_device(): sent = long_send.transpose(0, 2, 1).reshape(NX, NZ, NY, 2, NX, NZ, NY)  5.65 us
    unnamed x2, local copies, waits for them, and re-layouts  3.93 us

commit v1 on v0

--- a/solution.py
+++ b/solution.py
@@ -33,14 +33,14 @@
 def kernel(
     dims,
     count_ref,
-    senders_ref,
-    receivers_ref,
-    halo_ref,
-    pick_ref,
-    eg_ref,
-    eb_ref,
-    ng_ref,
-    nb_ref,
+    senders_hbm,
+    receivers_hbm,
+    halo_hbm,
+    eg_hbm,
+    eb_hbm,
+    ng_hbm,
+    nb_hbm,
+    long_hbm,
     node_hbm,
     edge_hbm,
     ef_hbm,
@@ -51,6 +51,14 @@
     edge_out,
     node_v,
     edge_v,
+    long_v,
+    senders_ref,
+    receivers_ref,
+    halo_ref,
+    eg_ref,
+    eb_ref,
+    ng_ref,
+    nb_ref,
     w1e,
     w2e,
     w1n,
@@ -70,6 +78,8 @@
     pre_v,
     hid_v,
     load_sem,
+    long_sem,
+    small_sem,
     out_sem,
     w_send,
     w_recv,
@@ -109,6 +119,27 @@
         pl.semaphore_signal(barrier, inc=1, device_id=p, device_id_type=MESH)
 
     weights = ((ef_hbm, w1e), (es_hbm, w2e), (nf_hbm, w1n), (ns_hbm, w2n))
+    long_load = [
+        pltpu.make_async_copy(
+            long_hbm.at[dom_of(x, i, y)], long_v.at[pl.ds(2 * i, 2)], long_sem.at[i]
+        )
+        for i in range(NZ)
+    ]
+    small = (
+        (senders_hbm, senders_ref),
+        (receivers_hbm, receivers_ref),
+        (halo_hbm, halo_ref),
+        (eg_hbm, eg_ref),
+        (eb_hbm, eb_ref),
+        (ng_hbm, ng_ref),
+        (nb_hbm, nb_ref),
+    )
+    small_load = [
+        pltpu.make_async_copy(src, dst, small_sem.at[i])
+        for i, (src, dst) in enumerate(small)
+    ]
+    for copy in small_load + long_load:
+        copy.start()
     node_load = pltpu.make_async_copy(node_hbm, node_v, load_sem.at[0])
     edge_load = pltpu.make_async_copy(edge_hbm, edge_v, load_sem.at[1])
     node_load.start()
@@ -122,6 +153,8 @@
             if l == 0 and i == 0:
                 edge_load.start()
 
+    for copy in small_load:
+        copy.wait()
     live = count_ref[0]
     table = lax.broadcasted_iota(jnp.int32, (K, E), 0)
     sent = senders_ref[...]
@@ -151,9 +184,28 @@
     o_pack[1] = jnp.where(row == col + COARSE, 1.0, 0.0).astype(BF16)
     o_halo = halo.astype(BF16)
     G = NX * NY * 2 * NZ
-    table = lax.broadcasted_iota(jnp.int32, (8 * NZ, G), 0)
-    o_pick[0] = jnp.where(table == pick_ref[...], 1.0, 0.0).T.astype(BF16)
-    o_pick[1] = jnp.where(table == pick_ref[...] + COARSE, 1.0, 0.0).T.astype(BF16)
+    row = lax.broadcasted_iota(jnp.int32, (G, nd), 0)
+    col = lax.broadcasted_iota(jnp.int32, (G, nd), 1)
+    to = lax.div(row, 2 * NZ)
+    want = dom_of(lax.div(to, NY), z, lax.rem(to, NY))
+    spread = jnp.where(col == want, 1.0, 0.0).astype(BF16)
+    for copy in long_load:
+        copy.wait()
+    coarse = long_v[...].astype(F32).astype(BF16)
+    every = lax.dot_general(
+        spread, coarse, (((1,), (1,)), ((), ())), preferred_element_type=F32
+    )
+    row = lax.broadcasted_iota(jnp.int32, (G, 2 * NZ), 0)
+    col = lax.broadcasted_iota(jnp.int32, (G, 2 * NZ), 1)
+    mine = jnp.where(col == lax.rem(row, 2 * NZ), every, 0.0).astype(BF16)
+    pick = dot(mine, jnp.ones((2 * NZ, 8 * NZ), BF16))
+    row = lax.broadcasted_iota(jnp.int32, (G, 8 * NZ), 0)
+    col = lax.broadcasted_iota(jnp.int32, (G, 8 * NZ), 1)
+    pick = pick + (8 * lax.div(lax.rem(row, 2 * NZ), 2)).astype(F32)
+    for h in range(2):
+        o_pick[h] = jnp.where(
+            col.astype(F32) == pick + float(COARSE * h), 1.0, 0.0
+        ).astype(BF16)
 
     def ring_copy(l, m, d):
         return pltpu.make_async_remote_copy(
@@ -381,17 +433,6 @@
     K = N + 2 * HALO
     F = 2 * nd
     G = NX * NY * 2 * NZ
-    dom = lax.axis_index("dom")
-    y = lax.rem(dom, NY)
-    z = lax.rem(lax.div(dom, NY), NZ)
-    x = lax.div(dom, NY * NZ)
-    sent = long_send.transpose(0, 2, 1).reshape(NX, NZ, NY, 2, NX, NZ, NY)
-    sent = lax.dynamic_slice(
-        sent, (x, 0, y, 0, 0, z, 0), (1, NZ, 1, 2, NX, 1, NY)
-    ).reshape(NZ, 2, NX * NY)
-    pick = sent.transpose(2, 0, 1) + 8 * jnp.arange(NZ, dtype=jnp.int32)[None, :, None]
-    pick = pick.reshape(1, G)
-    vmem = pl.BlockSpec(memory_space=pltpu.VMEM)
     smem = pl.BlockSpec(memory_space=pltpu.SMEM)
     hbm = pl.BlockSpec(memory_space=pl.ANY)
     DMA = pltpu.SemaphoreType.DMA
@@ -401,11 +442,19 @@
             jax.ShapeDtypeStruct((M, N, D), BF16),
             jax.ShapeDtypeStruct((M, E, D), BF16),
         ),
-        in_specs=[smem] + [vmem] * 8 + [hbm] * 6,
+        in_specs=[smem] + [hbm] * 14,
         out_specs=(hbm, hbm),
         scratch_shapes=[
             pltpu.VMEM((M, N, D), BF16),
             pltpu.VMEM((M, E, D), BF16),
+            pltpu.VMEM((2 * NZ, nd), jnp.int32),
+            pltpu.VMEM((1, E), jnp.int32),
+            pltpu.VMEM((1, E), jnp.int32),
+            pltpu.VMEM((1, 2 * HALO), jnp.int32),
+            pltpu.VMEM((L, D), F32),
+            pltpu.VMEM((L, D), F32),
+            pltpu.VMEM((L, D), F32),
+            pltpu.VMEM((L, D), F32),
             pltpu.VMEM((L, 2, 3 * D, H), BF16),
             pltpu.VMEM((L, 2, D, H), BF16),
             pltpu.VMEM((L, 2, 2 * D, H), BF16),
@@ -425,6 +474,8 @@
             pltpu.VMEM((M, E, D), F32),
             pltpu.VMEM((E, D), BF16),
             DMA((2 + 4 * L,)),
+            DMA((NZ,)),
+            DMA((7,)),
             DMA((M, 2)),
             DMA((L, 4)),
             DMA((L, 4)),
@@ -443,11 +494,11 @@
         edge_senders.reshape(1, E),
         edge_receivers.reshape(1, E),
         halo_send.reshape(1, 2 * HALO),
-        pick,
         edge_gain,
         edge_shift,
         node_gain,
         node_shift,
+        long_send.transpose(0, 2, 1),
         node_latents,
         edge_latents,
         edge_first,

time: 55.6 us -> 46.9 us (0.84)
  local copies, waits for them, and re-layouts: 12.5 us -> 3.93 us
    reshape x2 -> x0, local copies, waits for them, and re-layouts: 6.36 us -> none  [the longest x1 5.65 us: per_device(): sent = long_send.transpose(0, 2, 1).reshape(NX, NZ, NY, 2, NX, NZ, NY)]
    dynamic_slice x2 -> x0, local copies, waits for them, and re-layouts: 1.11 us -> none  [per_device(): lax.dynamic_slice(sent, (x, 0, y, 0, 0, z, 0), (1, NZ, 1, 2, NX, 1, NY))]
    transpose x1 -> x0, local copies, waits for them, and re-layouts: 0.91 us -> none  [per_device(): sent = long_send.transpose(0, 2, 1).reshape(NX, NZ, NY, 2, NX, NZ, NY)]
where the time goes in v1:
time: 46.9 us; the launch traced here: 46.7 us
  Pallas kernels  41.5 us (88%)
  local copies, waits for them, and re-layouts  3.93 us (8%)
  between operations  1.29 us (3%)
    pallas_call x1, Pallas kernels, per_device(): pl.pallas_call(functools.partial(kernel, (M, N, E, D)), out_shape=(jax.Sh...  41.5 us
    unnamed x2, local copies, waits for them, and re-layouts  3.93 us

profile of v1, /device:TPU:2, one launch (start us, length us, event | category | flops | bytes accessed | tf_op | source)
XLA Modules:
  0.0 46.7 jit_solution(18304801699327797336)
XLA Ops:
  1.3 41.5 %shard_map.158 = (bf16[2,128,512]{2,1,0:T(8,128)(2,1)}, bf16[2,512,512]{2,1,0:T(8,128)(2,1)}) custom-call(s32[1]{0:T(128)S(6)} %copy.19.count_ref, s32[1,512]{1,0:T(1,128)} %bitcast.5, s32[1,512]{1,0:T(1,128)} %bitcast.6, s32[1,32]{1,0:T(1,128)} %bitcast.7, f32[2,512]{1,0:T(2,128)} %eg_hbm.1, f32[2,512]{1,0:T(2,128)} %eb_hbm.1, f32[2,512]{1,0:T(2,128)} %ng_hbm.1, ...), custom_call_target="tpu_custom_call" | custom-call | tf_op jit(solution)/shard_map/pallas_call | solution.py:439
  42.8 1.7 %copy.20 = bf16[2,128,512]{2,1,0:T(8,128)(2,1)} copy(bf16[2,128,512]{2,1,0:T(8,128)(2,1)} %get-tuple-element.4) | data formatting | bytes 524288
  44.4 2.3 %copy.21 = bf16[2,512,512]{2,1,0:T(8,128)(2,1)} copy(bf16[2,512,512]{2,1,0:T(8,128)(2,1)} %get-tuple-element.5) | data formatting | bytes 2097152

commit v2 on v1

v2 whole, which is shorter than its diff:
```python
import functools

import jax
import jax.numpy as jnp
from jax import lax
from jax.experimental import pallas as pl
from jax.experimental.pallas import tpu as pltpu
from jax.sharding import PartitionSpec as P

NX, NZ, NY = 4, 8, 4
HALO = 16
LAYERS = 2
COARSE = 4
MESH = pl.DeviceIdType.MESH
F32 = jnp.float32
BF16 = jnp.bfloat16
RING = sorted(range(NZ), key=lambda d: (min(d, NZ - d), d))
BATCHES = (2, 1)
PLANE = sorted(
    [(i, j) for i in range(NX) for j in range(NY) if (i, j) != (0, 0)],
    key=lambda o: -(min(o[0], NX - o[0]) + min(o[1], NY - o[1])),
)


def dot(a, b):
    return jnp.dot(a, b, preferred_element_type=F32)


def silu(x):
    half = 0.5 * x
    return half * jnp.tanh(half) + half


def kernel(
    dims,
    count_hbm,
    senders_hbm,
    receivers_hbm,
    halo_hbm,
    eg_hbm,
    eb_hbm,
    ng_hbm,
    nb_hbm,
    long_hbm,
    node_hbm,
    edge_hbm,
    ef_hbm,
    es_hbm,
    nf_hbm,
    ns_hbm,
    node_out,
    edge_out,
    node_v,
    edge_v,
    head_v,
    long_v,
    count_ref,
    senders_ref,
    receivers_ref,
    halo_ref,
    eg_ref,
    eb_ref,
    ng_ref,
    nb_ref,
    w1e,
    w2e,
    w1n,
    w2n,
    near_rows,
    far_rows,
    ring_send,
    ring_recv,
    plane_send,
    halo_out,
    o_near,
    o_far,
    o_recv,
    o_sum,
    o_halo,
    o_pick_one,
    o_pick_two,
    pre_v,
    node_pre,
    hid_v,
    head_sem,
    load_sem,
    long_sem,
    small_sem,
    out_sem,
    w_send,
    w_recv,
    ring_ssem,
    ring_rsem,
    plane_ssem,
    plane_rsem,
    halo_ssem,
    halo_rsem,
):
    M, N, E, D = dims
    H = D // 2
    K = N + 2 * HALO
    dom = lax.axis_index("dom")
    mem = lax.axis_index("mem")
    y = lax.rem(dom, NY)
    z = lax.rem(lax.div(dom, NY), NZ)
    x = lax.div(dom, NY * NZ)

    def dom_of(a, b, c):
        return (a * NZ + b) * NY + c

    def along(d):
        return (dom_of(x, lax.rem(z + d, NZ), y), mem)

    def across(o):
        return (dom_of(lax.rem(x + o[0], NX), z, lax.rem(y + o[1], NY)), mem)

    nd = NX * NY * NZ
    after = (lax.rem(dom + 1, nd), mem)
    before = (lax.rem(dom + nd - 1, nd), mem)
    twin = (dom, 1 - mem)
    here = x * NY + y
    peers = [along(d) for d in RING[1:]] + [across(o) for o in PLANE]
    peers += [after, before, twin]
    barrier = pltpu.get_barrier_semaphore()
    for p in peers:
        pl.semaphore_signal(barrier, inc=1, device_id=p, device_id_type=MESH)

    weights = ((ef_hbm, w1e), (es_hbm, w2e), (nf_hbm, w1n), (ns_hbm, w2n))
    long_load = [
        pltpu.make_async_copy(
            long_hbm.at[dom_of(x, lax.rem(z + NZ - d, NZ), y)],
            long_v.at[pl.ds(2 * k, 2)],
            long_sem.at[k],
        )
        for k, d in enumerate(RING)
    ]
    small = (
        (count_hbm, count_ref),
        (senders_hbm, senders_ref),
        (receivers_hbm, receivers_ref),
        (halo_hbm, halo_ref),
        (eg_hbm, eg_ref),
        (eb_hbm, eb_ref),
        (ng_hbm, ng_ref),
        (nb_hbm, nb_ref),
    )
    small_load = [
        pltpu.make_async_copy(src, dst, small_sem.at[i])
        for i, (src, dst) in enumerate(small)
    ]
    for copy in small_load + long_load:
        copy.start()
    node_load = pltpu.make_async_copy(node_hbm, node_v, load_sem.at[0])
    edge_load = pltpu.make_async_copy(edge_hbm, edge_v, load_sem.at[1])
    head_load = pltpu.make_async_copy(node_hbm.at[:, pl.ds(0, 8)], head_v, head_sem)
    head_load.start()
    node_load.start()
    w_load = {}
    for l in range(LAYERS):
        for i, (src, dst) in enumerate(weights):
            w_load[l, i] = pltpu.make_async_copy(
                src.at[l], dst.at[l, mem], load_sem.at[2 + 4 * l + i]
            )
            w_load[l, i].start()
            if l == 0 and i == 0:
                edge_load.start()

    F = 2 * nd

    def ring_copy(l, m, k):
        return pltpu.make_async_remote_copy(
            src_ref=ring_send.at[l, m],
            dst_ref=ring_recv.at[l, m, k],
            send_sem=ring_ssem.at[l, m, k],
            recv_sem=ring_rsem.at[l, m, k],
            device_id=along(RING[k]),
            device_id_type=MESH,
        )

    def plane_copy(l, m, b, k):
        o = PLANE[k]
        there = lax.rem(x + o[0], NX) * NY + lax.rem(y + o[1], NY)
        rows = 2 * NZ // BATCHES[l]
        return pltpu.make_async_remote_copy(
            src_ref=plane_send.at[l, m, there, pl.ds(b * rows, rows)],
            dst_ref=far_rows.at[l, m, here, pl.ds(b * rows, rows)],
            send_sem=plane_ssem.at[l, m, b, k],
            recv_sem=plane_rsem.at[l, m, b, k],
            device_id=across(o),
            device_id_type=MESH,
        )

    def halo_copy(l, m, side):
        return pltpu.make_async_remote_copy(
            src_ref=halo_out.at[l, m, side],
            dst_ref=near_rows.at[l, m, pl.ds(N + (1 - side) * HALO, HALO)],
            send_sem=halo_ssem.at[l, m, side],
            recv_sem=halo_rsem.at[l, m, side],
            device_id=before if side == 0 else after,
            device_id_type=MESH,
        )

    def weight_copy(l, i):
        src, dst = weights[i]
        return pltpu.make_async_remote_copy(
            src_ref=src.at[l],
            dst_ref=dst.at[l, mem],
            send_sem=w_send.at[l, i],
            recv_sem=w_recv.at[l, i],
            device_id=twin,
            device_id_type=MESH,
        )

    def pack(l, m, rows):
        wide = rows.astype(F32)
        upper = pltpu.roll(wide[:, H:D], COARSE, 0)
        row = lax.broadcasted_iota(jnp.int32, (8, H), 0)
        packed = jnp.where(row < COARSE, wide[:, 0:H], upper).astype(BF16)
        ring_send[l, m] = packed
        ring_recv[l, m, 0] = packed

    def halo_pack(l, m, rows):
        out = dot(o_halo[...], rows).astype(BF16)
        halo_out[l, m, 0] = out[0:HALO]
        halo_out[l, m, 1] = out[HALO : 2 * HALO]

    def ring_start(l, m):
        for k in reversed(range(1, NZ)):
            ring_copy(l, m, k).start()

    def halo_start(l, m):
        for side in range(2):
            halo_copy(l, m, side).start()

    def forward(l, m, b):
        nb = BATCHES[l]
        o_pick = o_pick_one if nb == 1 else o_pick_two
        size = NZ // nb
        for k in range(max(b * size, 1), (b + 1) * size):
            ring_copy(l, m, k).wait_recv()
        got = ring_recv[l, m, b * size : (b + 1) * size].reshape(8 * size, H)
        S = 2 * size
        rows = slice(b * NX * NY * S, (b + 1) * NX * NY * S)
        for h in range(2):
            plane_send[l, m, :, b * S : (b + 1) * S, h * H : (h + 1) * H] = (
                dot(o_pick[h, rows], got).astype(BF16).reshape(NX * NY, S, H)
            )
        for k in range(len(PLANE)):
            plane_copy(l, m, b, k).start()
        far_rows[l, m, here, b * S : (b + 1) * S] = plane_send[
            l, m, here, b * S : (b + 1) * S
        ]

    def halo_wait(l, m):
        for side in range(2):
            halo_copy(l, m, side).wait_recv()

    def own_part(l, m):
        rows = near_rows[l, m, 0:N]
        for n in range(2):
            cols = slice(n * H, (n + 1) * H)
            own = dot(rows, w1e[l, n, 2 * D : 3 * D]).astype(BF16)
            pre_v[m, :, cols] = dot(edge_v[m], w1e[l, n, 0:D]) + dot(o_recv[...], own)

    def near_part(l, m):
        rows = near_rows[l, m]
        for n in range(2):
            cols = slice(n * H, (n + 1) * H)
            proj = dot(rows, w1e[l, n, D : 2 * D]).astype(BF16)
            pre_v[m, :, cols] += dot(o_near[...], proj)

    def node_part(l, m):
        rows = near_rows[l, m, 0:N]
        for n in range(2):
            node_pre[m, :, n * H : (n + 1) * H] = dot(rows, w1n[l, n, 0:D])

    def norm(v, gain, shift):
        mean = jnp.mean(v, -1, keepdims=True)
        c = v - mean
        var = jnp.mean(c * c, -1, keepdims=True)
        return c * lax.rsqrt(var + 1e-05) * gain + shift

    CH = min(256, E)

    def edges(l, m):
        for b in range(BATCHES[l]):
            for k in range(len(PLANE)):
                plane_copy(l, m, b, k).wait_recv()
        rows = far_rows[l, m].reshape(F, D)
        for n in range(2):
            cols = slice(n * H, (n + 1) * H)
            proj = dot(rows, w1e[l, n, D : 2 * D]).astype(BF16)
            for c in range(E // CH):
                r = slice(c * CH, (c + 1) * CH)
                hid_v[r, cols] = silu(pre_v[m, r, cols] + dot(o_far[r], proj)).astype(BF16)
        gain = eg_ref[l : l + 1]
        shift = eb_ref[l : l + 1]
        for c in range(E // CH):
            r = slice(c * CH, (c + 1) * CH)
            h = hid_v[r]
            v = jnp.concatenate([dot(h, w2e[l, 0]), dot(h, w2e[l, 1])], -1)
            u = norm(v, gain, shift)
            at = lax.broadcasted_iota(jnp.int32, (CH, 1), 0) + c * CH
            edge_v[m, r] = jnp.where(
                at < live, edge_v[m, r].astype(F32) + u, 0.0
            ).astype(BF16)

    def nodes(l, m):
        summed = dot(o_sum[...], edge_v[m]).astype(BF16)
        rows = near_rows[l, m, 0:N]
        hid = []
        for n in range(2):
            a = node_pre[m, :, n * H : (n + 1) * H] + dot(summed, w1n[l, n, D : 2 * D])
            hid.append(silu(a).astype(BF16))
        h = jnp.concatenate(hid, -1)
        v = jnp.concatenate([dot(h, w2n[l, 0]), dot(h, w2n[l, 1])], -1)
        u = norm(v, ng_ref[l : l + 1], nb_ref[l : l + 1])
        return (rows.astype(F32) + u).astype(BF16)

    head_load.wait()
    for m in range(M):
        pack(0, m, head_v[m])
    pl.semaphore_wait(barrier, len(peers))
    for m in range(M):
        ring_start(0, m)
    for copy in small_load:
        copy.wait()
    row = lax.broadcasted_iota(jnp.int32, (N, 2 * HALO), 0)
    halo = jnp.where(row == halo_ref[...], 1.0, 0.0).T
    o_halo[...] = halo.astype(BF16)
    node_load.wait()
    for m in range(M):
        rows = node_v[m]
        near_rows[0, m, 0:N] = rows
        halo_pack(0, m, rows)
        halo_start(0, m)
    for l in range(LAYERS):
        for i in range(4):
            weight_copy(l, i).start()
    for copy in long_load:
        copy.wait()
    coarse = long_v[...].astype(F32).astype(BF16)
    G = NX * NY * 2 * NZ
    for nb, o_pick in ((1, o_pick_one), (2, o_pick_two)):
        S = 2 * NZ // nb
        row = lax.broadcasted_iota(jnp.int32, (G, nd), 0)
        col = lax.broadcasted_iota(jnp.int32, (G, nd), 1)
        to = lax.rem(lax.div(row, S), NX * NY)
        want = dom_of(lax.div(to, NY), z, lax.rem(to, NY))
        spread = jnp.where(col == want, 1.0, 0.0).astype(BF16)
        every = lax.dot_general(
            spread, coarse, (((1,), (1,)), ((), ())), preferred_element_type=F32
        )
        row = lax.broadcasted_iota(jnp.int32, (G, 2 * NZ), 0)
        col = lax.broadcasted_iota(jnp.int32, (G, 2 * NZ), 1)
        own = lax.div(row, NX * NY * S) * S + lax.rem(row, S)
        mine = jnp.where(col == own, every, 0.0).astype(BF16)
        pick = dot(mine, jnp.ones((2 * NZ, 4 * S), BF16))
        row = lax.broadcasted_iota(jnp.int32, (G, 4 * S), 0)
        col = lax.broadcasted_iota(jnp.int32, (G, 4 * S), 1)
        pick = pick + (8 * lax.div(lax.rem(row, S), 2)).astype(F32)
        for h in range(2):
            o_pick[h] = jnp.where(
                col.astype(F32) == pick + float(COARSE * h), 1.0, 0.0
            ).astype(BF16)

    live = count_ref[0]
    table = lax.broadcasted_iota(jnp.int32, (K, E), 0)
    sent = senders_ref[...]
    o_near[...] = jnp.where(table == sent, 1.0, 0.0).T.astype(BF16)
    q = jnp.maximum(sent - K, 0)
    slot = lax.rem(q, 2)
    part = lax.div(q, 2)
    part_y = lax.rem(part, NY)
    part_z = lax.rem(lax.div(part, NY), NZ)
    part_x = lax.div(part, NY * NZ)
    apart = lax.rem(z + NZ - part_z, NZ)
    rank = jnp.zeros_like(apart)
    for k, d in enumerate(RING):
        rank = jnp.where(apart == d, k, rank)
    place = (part_x * NY + part_y) * (2 * NZ) + rank * 2 + slot
    place = jnp.where(sent >= K, place, -1)
    table = lax.broadcasted_iota(jnp.int32, (F, E), 0)
    o_far[...] = jnp.where(table == place, 1.0, 0.0).T.astype(BF16)
    table = lax.broadcasted_iota(jnp.int32, (N, E), 0)
    lane = lax.broadcasted_iota(jnp.int32, (N, E), 1)
    got = jnp.where((table == receivers_ref[...]) & (lane < live), 1.0, 0.0)
    o_sum[...] = got.astype(BF16)
    o_recv[...] = got.T.astype(BF16)
    for b in range(BATCHES[0]):
        for m in range(M):
            forward(0, m, b)
    edge_load.wait()
    for i in range(4):
        w_load[0, i].wait()
    weight_copy(0, 0).wait_recv()
    for m in range(M):
        own_part(0, m)
    for m in range(M):
        halo_wait(0, m)
        near_part(0, m)
    for i in range(1, 4):
        weight_copy(0, i).wait_recv()
    for m in range(M):
        node_part(0, m)
    for m in range(M):
        edges(0, m)
        new = nodes(0, m)
        pack(1, m, new[0:8])
        ring_start(1, m)
        near_rows[1, m, 0:N] = new
        halo_pack(1, m, new)
        halo_start(1, m)
    for i in range(4):
        w_load[1, i].wait()
        weight_copy(1, i).wait_recv()
    own_part(1, 0)
    forward(1, 0, 0)
    own_part(1, 1)
    node_part(1, 0)
    forward(1, 1, 0)
    node_part(1, 1)
    halo_wait(1, 0)
    near_part(1, 0)
    halo_wait(1, 1)
    near_part(1, 1)
    outs = []
    for m in range(M):
        edges(1, m)
        out = pltpu.make_async_copy(edge_v.at[m], edge_out.at[m], out_sem.at[m, 0])
        out.start()
        outs.append(out)
        node_v[m] = nodes(1, m)
        out = pltpu.make_async_copy(node_v.at[m], node_out.at[m], out_sem.at[m, 1])
        out.start()
        outs.append(out)
    for l in range(LAYERS):
        for i in range(4):
            weight_copy(l, i).wait_send()
        for m in range(M):
            for k in range(1, NZ):
                ring_copy(l, m, k).wait_send()
            for b in range(BATCHES[l]):
                for k in range(len(PLANE)):
                    plane_copy(l, m, b, k).wait_send()
            for side in range(2):
                halo_copy(l, m, side).wait_send()
    for out in outs:
        out.wait()


def publish(node_in, edge_in, node_out, edge_out, node_v, edge_v, in_sem, out_sem):
    M, E = edge_in.shape[:2]
    pieces = []
    for m in range(M):
        for h in range(2):
            rows = pl.ds(h * (E // 2), E // 2)
            pieces.append(
                (edge_in.at[m, rows], edge_v.at[2 * m + h], edge_out.at[m, rows])
            )
    pieces.append((node_in, node_v, node_out))
    ins = [
        pltpu.make_async_copy(a, b, in_sem.at[i]) for i, (a, b, c) in enumerate(pieces)
    ]
    outs = [
        pltpu.make_async_copy(b, c, out_sem.at[i]) for i, (a, b, c) in enumerate(pieces)
    ]
    for copy in ins:
        copy.start()
    for a, b in zip(ins, outs):
        a.wait()
        b.start()
    for copy in outs:
        copy.wait()


def per_device(
    node_latents,
    edge_latents,
    edge_senders,
    edge_receivers,
    edge_counts,
    halo_send,
    long_send,
    edge_first,
    edge_second,
    node_first,
    node_second,
    edge_gain,
    edge_shift,
    node_gain,
    node_shift,
):
    M, N, D = node_latents.shape
    E = edge_latents.shape[1]
    H = D // 2
    L = LAYERS
    nd = NX * NY * NZ
    K = N + 2 * HALO
    F = 2 * nd
    G = NX * NY * 2 * NZ
    hbm = pl.BlockSpec(memory_space=pl.ANY)
    DMA = pltpu.SemaphoreType.DMA
    node_state, edge_state = pl.pallas_call(
        functools.partial(kernel, (M, N, E, D)),
        out_shape=(
            jax.ShapeDtypeStruct((M, N, D), BF16),
            jax.ShapeDtypeStruct((M, E, D), BF16),
        ),
        in_specs=[hbm] * 15,
        out_specs=(hbm, hbm),
        scratch_shapes=[
            pltpu.VMEM((M, N, D), BF16),
            pltpu.VMEM((M, E, D), BF16),
            pltpu.VMEM((M, 8, D), BF16),
            pltpu.VMEM((2 * NZ, nd), jnp.int32),
            pltpu.SMEM((1,), jnp.int32),
            pltpu.VMEM((1, E), jnp.int32),
            pltpu.VMEM((1, E), jnp.int32),
            pltpu.VMEM((1, 2 * HALO), jnp.int32),
            pltpu.VMEM((L, D), F32),
            pltpu.VMEM((L, D), F32),
            pltpu.VMEM((L, D), F32),
            pltpu.VMEM((L, D), F32),
            pltpu.VMEM((L, 2, 3 * D, H), BF16),
            pltpu.VMEM((L, 2, D, H), BF16),
            pltpu.VMEM((L, 2, 2 * D, H), BF16),
            pltpu.VMEM((L, 2, D, H), BF16),
            pltpu.VMEM((L, M, K, D), BF16),
            pltpu.VMEM((L, M, NX * NY, 2 * NZ, D), BF16),
            pltpu.VMEM((L, M, 8, H), BF16),
            pltpu.VMEM((L, M, NZ, 8, H), BF16),
            pltpu.VMEM((L, M, NX * NY, 2 * NZ, D), BF16),
            pltpu.VMEM((L, M, 2, HALO, D), BF16),
            pltpu.VMEM((E, K), BF16),
            pltpu.VMEM((E, F), BF16),
            pltpu.VMEM((E, N), BF16),
            pltpu.VMEM((N, E), BF16),
            pltpu.VMEM((2 * HALO, N), BF16),
            pltpu.VMEM((2, G, 8 * NZ), BF16),
            pltpu.VMEM((2, G, 4 * NZ), BF16),
            pltpu.VMEM((M, E, D), F32),
            pltpu.VMEM((M, N, D), F32),
            pltpu.VMEM((E, D), BF16),
            DMA(()),
            DMA((2 + 4 * L,)),
            DMA((NZ,)),
            DMA((8,)),
            DMA((M, 2)),
            DMA((L, 4)),
            DMA((L, 4)),
            DMA((L, M, NZ)),
            DMA((L, M, NZ)),
            DMA((L, M, 2, len(PLANE))),
            DMA((L, M, 2, len(PLANE))),
            DMA((L, M, 2)),
            DMA((L, M, 2)),
        ],
        compiler_params=pltpu.CompilerParams(
            collective_id=0, has_side_effects=True, vmem_limit_bytes=56 * 1024 * 1024
        ),
    )(
        edge_counts,
        edge_senders.reshape(1, E),
        edge_receivers.reshape(1, E),
        halo_send.reshape(1, 2 * HALO),
        edge_gain,
        edge_shift,
        node_gain,
        node_shift,
        long_send.transpose(0, 2, 1),
        node_latents,
        edge_latents,
        edge_first,
        edge_second,
        node_first,
        node_second,
    )
    return pl.pallas_call(
        publish,
        out_shape=(
            jax.ShapeDtypeStruct((M, N, D), BF16),
            jax.ShapeDtypeStruct((M, E, D), BF16),
        ),
        in_specs=[hbm, hbm],
        out_specs=(hbm, hbm),
        scratch_shapes=[
            pltpu.VMEM((M, N, D), BF16),
            pltpu.VMEM((2 * M, E // 2, D), BF16),
            DMA((1 + 2 * M,)),
            DMA((1 + 2 * M,)),
        ],
    )(node_state, edge_state)


def solution(mesh):
    placed = (
        P("mem", "dom", None),
        P("mem", "dom", None),
        P("dom"),
        P("dom"),
        P("dom"),
        P("dom"),
        P(),
        P(None, None, "mem"),
        P(None, None, "mem"),
        P(None, None, "mem"),
        P(None, None, "mem"),
        P(),
        P(),
        P(),
        P(),
    )
    return jax.shard_map(
        per_device,
        mesh=mesh,
        in_specs=placed,
        out_specs=(P("mem", "dom", None), P("mem", "dom", None)),
        check_vma=False,
    )
```

time: 46.9 us -> 43.6 us (0.930)
  local copies, waits for them, and re-layouts: 3.93 us -> 0 us
  Pallas kernels: 41.5 us -> 42 us
    unnamed x2 -> x0, local copies, waits for them, and re-layouts: 3.93 us -> none
    pallas_call x0 -> x1, Pallas kernels: none -> 2.08 us  [per_device(): pl.pallas_call(publish, out_shape=(jax.ShapeDtypeStruct((M, N, D), BF16),...]
    pallas_call x1, Pallas kernels: 41.5 us -> 40 us  [per_device(): pl.pallas_call(functools.partial(kernel, (M, N, E, D)), out_shape=(jax.Sh...]
where the time goes in v2:
time: 43.6 us; the launch traced here: 43.3 us
  Pallas kernels  42 us (96%)
  between operations  1.29 us (3%)
    pallas_call x1, Pallas kernels, per_device(): pl.pallas_call(functools.partial(kernel, (M, N, E, D)), out_shape=(jax.Sh...  40 us
    pallas_call x1, Pallas kernels, per_device(): pl.pallas_call(publish, out_shape=(jax.ShapeDtypeStruct((M, N, D), BF16),...  2.08 us

profile of v2, /device:TPU:2, one launch (start us, length us, event | category | flops | bytes accessed | tf_op | source)
XLA Modules:
  0.0 43.3 jit_solution(6059747977586891993)
XLA Ops:
  1.3 40.0 %shard_map.158 = (bf16[2,128,512]{2,1,0:T(8,128)(2,1)}, bf16[2,512,512]{2,1,0:T(8,128)(2,1)}) custom-call(s32[1]{0:T(128)S(6)} %copy.17.count_hbm, s32[1,512]{1,0:T(1,128)} %bitcast.5, s32[1,512]{1,0:T(1,128)} %bitcast.6, s32[1,32]{1,0:T(1,128)} %bitcast.7, f32[2,512]{1,0:T(2,128)} %eg_hbm.1, f32[2,512]{1,0:T(2,128)} %eb_hbm.1, f32[2,512]{1,0:T(2,128)} %ng_hbm.1, ...), custom_call_target="tpu_custom_call" | custom-call | tf_op jit(solution)/shard_map/pallas_call | solution.py:504
  41.2 2.1 %shard_map.159 = (bf16[2,128,512]{2,1,0:T(8,128)(2,1)}, bf16[2,512,512]{2,1,0:T(8,128)(2,1)}) custom-call(bf16[2,128,512]{2,1,0:T(8,128)(2,1)} %get-tuple-element.4.node_in, bf16[2,512,512]{2,1,0:T(8,128)(2,1)} %get-tuple-element.5.edge_in), custom_call_target="tpu_custom_call" | custom-call | tf_op jit(solution)/shard_map/pallas_call | solution.py:579

commit v3 on v2

--- a/solution.py
+++ b/solution.py
@@ -275,10 +275,14 @@
             node_pre[m, :, n * H : (n + 1) * H] = dot(rows, w1n[l, n, 0:D])
 
     def norm(v, gain, shift):
-        mean = jnp.mean(v, -1, keepdims=True)
-        c = v - mean
-        var = jnp.mean(c * c, -1, keepdims=True)
-        return c * lax.rsqrt(var + 1e-05) * gain + shift
+        var = jnp.mean(v * v, -1, keepdims=True)
+        return v * lax.rsqrt(var + 1e-05) * gain + shift
+
+    def centre(l, w):
+        a, b = w[l, 0].astype(F32), w[l, 1].astype(F32)
+        mean = jnp.sum(a + b, -1, keepdims=True) * (1.0 / D)
+        w[l, 0] = (a - mean).astype(BF16)
+        w[l, 1] = (b - mean).astype(BF16)
 
     CH = min(256, E)
 
@@ -401,29 +405,33 @@
         near_part(0, m)
     for i in range(1, 4):
         weight_copy(0, i).wait_recv()
+    centre(0, w2e)
+    centre(0, w2n)
     for m in range(M):
         node_part(0, m)
+    for i in range(4):
+        w_load[1, i].wait()
+        weight_copy(1, i).wait_recv()
+    centre(1, w2e)
+    centre(1, w2n)
     for m in range(M):
         edges(0, m)
         new = nodes(0, m)
         pack(1, m, new[0:8])
         ring_start(1, m)
         near_rows[1, m, 0:N] = new
-        halo_pack(1, m, new)
+    for m in range(M):
+        halo_pack(1, m, near_rows[1, m, 0:N])
         halo_start(1, m)
-    for i in range(4):
-        w_load[1, i].wait()
-        weight_copy(1, i).wait_recv()
     own_part(1, 0)
-    forward(1, 0, 0)
     own_part(1, 1)
     node_part(1, 0)
+    node_part(1, 1)
+    forward(1, 0, 0)
     forward(1, 1, 0)
-    node_part(1, 1)
-    halo_wait(1, 0)
-    near_part(1, 0)
-    halo_wait(1, 1)
-    near_part(1, 1)
+    for m in range(M):
+        halo_wait(1, m)
+        near_part(1, m)
     outs = []
     for m in range(M):
         edges(1, m)

time: 43.6 us -> 42.9 us (0.984)
  Pallas kernels: 42 us -> 41.3 us
    pallas_call x1, Pallas kernels: 40 us -> 39.2 us  [per_device(): pl.pallas_call(functools.partial(kernel, (M, N, E, D)), out_shape=(jax.Sh...]
where the time goes in v3:
time: 42.9 us; the launch traced here: 42.6 us
  Pallas kernels  41.3 us (96%)
  between operations  1.29 us (3%)
    pallas_call x1, Pallas kernels, per_device(): pl.pallas_call(functools.partial(kernel, (M, N, E, D)), out_shape=(jax.Sh...  39.2 us
    pallas_call x1, Pallas kernels, per_device(): pl.pallas_call(publish, out_shape=(jax.ShapeDtypeStruct((M, N, D), BF16),...  2.08 us

profile of v3, /device:TPU:2, one launch (start us, length us, event | category | flops | bytes accessed | tf_op | source)
XLA Modules:
  0.0 42.6 jit_solution(15314956935201238511)
XLA Ops:
  1.3 39.2 %shard_map.158 = (bf16[2,128,512]{2,1,0:T(8,128)(2,1)}, bf16[2,512,512]{2,1,0:T(8,128)(2,1)}) custom-call(s32[1]{0:T(128)S(6)} %copy.17.count_hbm, s32[1,512]{1,0:T(1,128)} %bitcast.5, s32[1,512]{1,0:T(1,128)} %bitcast.6, s32[1,32]{1,0:T(1,128)} %bitcast.7, f32[2,512]{1,0:T(2,128)} %eg_hbm.1, f32[2,512]{1,0:T(2,128)} %eb_hbm.1, f32[2,512]{1,0:T(2,128)} %ng_hbm.1, ...), custom_call_target="tpu_custom_call" | custom-call | tf_op jit(solution)/shard_map/pallas_call | solution.py:512
  40.5 2.1 %shard_map.159 = (bf16[2,128,512]{2,1,0:T(8,128)(2,1)}, bf16[2,512,512]{2,1,0:T(8,128)(2,1)}) custom-call(bf16[2,128,512]{2,1,0:T(8,128)(2,1)} %get-tuple-element.4.node_in, bf16[2,512,512]{2,1,0:T(8,128)(2,1)} %get-tuple-element.5.edge_in), custom_call_target="tpu_custom_call" | custom-call | tf_op jit(solution)/shard_map/pallas_call | solution.py:587

commit v4 on v3

--- a/solution.py
+++ b/solution.py
@@ -318,8 +318,12 @@
             hid.append(silu(a).astype(BF16))
         h = jnp.concatenate(hid, -1)
         v = jnp.concatenate([dot(h, w2n[l, 0]), dot(h, w2n[l, 1])], -1)
-        u = norm(v, ng_ref[l : l + 1], nb_ref[l : l + 1])
-        return (rows.astype(F32) + u).astype(BF16)
+        gain = ng_ref[l : l + 1]
+        shift = nb_ref[l : l + 1]
+        if l + 1 < LAYERS:
+            pack(l + 1, m, (rows[0:8].astype(F32) + norm(v[0:8], gain, shift)).astype(BF16))
+            ring_start(l + 1, m)
+        return (rows.astype(F32) + norm(v, gain, shift)).astype(BF16)
 
     head_load.wait()
     for m in range(M):
@@ -417,8 +421,6 @@
     for m in range(M):
         edges(0, m)
         new = nodes(0, m)
-        pack(1, m, new[0:8])
-        ring_start(1, m)
         near_rows[1, m, 0:N] = new
     for m in range(M):
         halo_pack(1, m, near_rows[1, m, 0:N])

time: 42.9 us -> 42.9 us (level)
  no operation moved by 1% of the time
where the time goes in v4:
time: 42.9 us; the launch traced here: 42.6 us
  Pallas kernels  41.3 us (96%)
  between operations  1.29 us (3%)
    pallas_call x1, Pallas kernels, per_device(): pl.pallas_call(functools.partial(kernel, (M, N, E, D)), out_shape=(jax.Sh...  39.2 us
    pallas_call x1, Pallas kernels, per_device(): pl.pallas_call(publish, out_shape=(jax.ShapeDtypeStruct((M, N, D), BF16),...  2.08 us

profile of v4, /device:TPU:2, one launch (start us, length us, event | category | flops | bytes accessed | tf_op | source)
XLA Modules:
  0.0 42.6 jit_solution(1439033460718471871)
XLA Ops:
  1.3 39.2 %shard_map.158 = (bf16[2,128,512]{2,1,0:T(8,128)(2,1)}, bf16[2,512,512]{2,1,0:T(8,128)(2,1)}) custom-call(s32[1]{0:T(128)S(6)} %copy.17.count_hbm, s32[1,512]{1,0:T(1,128)} %bitcast.5, s32[1,512]{1,0:T(1,128)} %bitcast.6, s32[1,32]{1,0:T(1,128)} %bitcast.7, f32[2,512]{1,0:T(2,128)} %eg_hbm.1, f32[2,512]{1,0:T(2,128)} %eb_hbm.1, f32[2,512]{1,0:T(2,128)} %ng_hbm.1, ...), custom_call_target="tpu_custom_call" | custom-call | tf_op jit(solution)/shard_map/pallas_call | solution.py:514
  40.5 2.1 %shard_map.159 = (bf16[2,128,512]{2,1,0:T(8,128)(2,1)}, bf16[2,512,512]{2,1,0:T(8,128)(2,1)}) custom-call(bf16[2,128,512]{2,1,0:T(8,128)(2,1)} %get-tuple-element.4.node_in, bf16[2,512,512]{2,1,0:T(8,128)(2,1)} %get-tuple-element.5.edge_in), custom_call_target="tpu_custom_call" | custom-call | tf_op jit(solution)/shard_map/pallas_call | solution.py:589

commit v5 on v4

--- a/solution.py
+++ b/solution.py
@@ -372,6 +372,9 @@
                 col.astype(F32) == pick + float(COARSE * h), 1.0, 0.0
             ).astype(BF16)
 
+    for b in range(BATCHES[0]):
+        for m in range(M):
+            forward(0, m, b)
     live = count_ref[0]
     table = lax.broadcasted_iota(jnp.int32, (K, E), 0)
     sent = senders_ref[...]
@@ -395,9 +398,6 @@
     got = jnp.where((table == receivers_ref[...]) & (lane < live), 1.0, 0.0)
     o_sum[...] = got.astype(BF16)
     o_recv[...] = got.T.astype(BF16)
-    for b in range(BATCHES[0]):
-        for m in range(M):
-            forward(0, m, b)
     edge_load.wait()
     for i in range(4):
         w_load[0, i].wait()

time: 42.9 us -> 42.9 us (level)
  no operation moved by 1% of the time
where the time goes in v5:
time: 42.9 us; the launch traced here: 42.6 us
  Pallas kernels  41.3 us (96%)
  between operations  1.29 us (3%)
    pallas_call x1, Pallas kernels, per_device(): pl.pallas_call(functools.partial(kernel, (M, N, E, D)), out_shape=(jax.Sh...  39.2 us
    pallas_call x1, Pallas kernels, per_device(): pl.pallas_call(publish, out_shape=(jax.ShapeDtypeStruct((M, N, D), BF16),...  2.08 us

profile of v5, /device:TPU:2, one launch (start us, length us, event | category | flops | bytes accessed | tf_op | source)
XLA Modules:
  0.0 42.6 jit_solution(15860520752215490789)
XLA Ops:
  1.3 39.2 %shard_map.158 = (bf16[2,128,512]{2,1,0:T(8,128)(2,1)}, bf16[2,512,512]{2,1,0:T(8,128)(2,1)}) custom-call(s32[1]{0:T(128)S(6)} %copy.17.count_hbm, s32[1,512]{1,0:T(1,128)} %bitcast.5, s32[1,512]{1,0:T(1,128)} %bitcast.6, s32[1,32]{1,0:T(1,128)} %bitcast.7, f32[2,512]{1,0:T(2,128)} %eg_hbm.1, f32[2,512]{1,0:T(2,128)} %eb_hbm.1, f32[2,512]{1,0:T(2,128)} %ng_hbm.1, ...), custom_call_target="tpu_custom_call" | custom-call | tf_op jit(solution)/shard_map/pallas_call | solution.py:514
  40.5 2.1 %shard_map.159 = (bf16[2,128,512]{2,1,0:T(8,128)(2,1)}, bf16[2,512,512]{2,1,0:T(8,128)(2,1)}) custom-call(bf16[2,128,512]{2,1,0:T(8,128)(2,1)} %get-tuple-element.4.node_in, bf16[2,512,512]{2,1,0:T(8,128)(2,1)} %get-tuple-element.5.edge_in), custom_call_target="tpu_custom_call" | custom-call | tf_op jit(solution)/shard_map/pallas_call | solution.py:589
